TPU v7x, 256 devices: a whole 4x4x8 slice. The times are simulated.
256 devices in a mesh: band: 32 (over z, y_hi, core), chan: 8 (over x, y_lo).
Axes of the slice: x: 4, y: 4 (y_hi: 2, y_lo: 2; y = y_hi * 2 + y_lo), z: 8, core: 2. Of those that a mesh axis runs over, the one named last changes fastest.
Arguments:
- fine_features: bfloat16 [2, 192, 256, 512], P(None, 'chan', 'band'), may hold values from -100 to 100
- coarse_level: bfloat16 [2, 256, 128, 256], P(None, 'chan', 'band'), may hold values from -100 to 100
- lat_weight: bfloat16 [256, 192], P('chan'), may hold values from -0.4375 to 0.4375
- lat_gain: bfloat16 [256], P('chan'), may hold values from 0.099609375 to 1.8984375
- lat_shift: bfloat16 [256], P('chan'), may hold values from -3 to 3
- out_weight: bfloat16 [3, 3, 256, 256], P(None, None, 'chan'), may hold values from -0.125 to 0.125
- out_gain: bfloat16 [256], P('chan'), may hold values from 0.099609375 to 1.8984375
- out_shift: bfloat16 [256], P('chan'), may hold values from -3 to 3
- mask_weight: bfloat16 [256, 256], P('chan'), may hold values from -0.375 to 0.375
- mask_bias: bfloat16 [256], P('chan'), may hold values from -1.796875 to 1.796875
- queries: bfloat16 [200, 256], replicated, may hold values from -128 to 128
Outputs:
- log_probs: float32 [2, 200, 256, 512], P(None, None, ('band', 'chan'))
All inputs are finite; a program needn't handle non-finite values.
Results may differ from a plain program's by a relative error of at most 0.0058.
Values may be sent and summed in bfloat16 or wider, within the bound.
A program may use at most 64 MiB of HBM per device.

v0:
```python
import functools
import jax
import jax.numpy as jnp
from jax import lax
from jax.sharding import Mesh
from jax.sharding import PartitionSpec as P

D = 256
GROUPS = 32
BAND = ("band_0", "band_1", "band_2")
CHAN = ("chan_0", "chan_1")
BAND_CHAN = ("band_0", "band_1", "band_2", "chan_0", "chan_1")
epsilon = 1e-05


def whole_of(shard, axes, dim):
    for axis in reversed(axes):
        shard = lax.all_gather(shard, axis, axis=dim, tiled=True)
    return shard


def from_everyone(shard, axis):
    devices = lax.axis_size(axis)
    return lax.all_to_all(
        jnp.broadcast_to(shard[None], (devices, *shard.shape)), axis, 0, 0, tiled=True
    )


def of_everyone(shard, axis):
    everything = from_everyone(shard, axis)
    return jnp.sum(everything, axis=0)


def together(arrays, axis):
    vector, at, done = (jnp.concatenate([a.reshape(-1) for a in arrays]), 0, [])
    total = of_everyone(vector, axis)
    for a in arrays:
        done.append(total[at : at + a.size].reshape(a.shape))
        at += a.size
    return tuple(done)


def extended_2(cells, sides, width):
    for axis, dim in sides:
        count = lax.axis_size(axis)
        ends = count - 1
        head = lax.slice_in_dim(cells, 0, width, axis=dim)
        tail = lax.slice_in_dim(cells, cells.shape[dim] - width, cells.shape[dim], axis=dim)
        cells = jnp.concatenate(
            [
                lax.ppermute(tail, axis, [(i, (i + 1) % count) for i in range(ends)]),
                cells,
                lax.ppermute(head, axis, [((i + 1) % count, i) for i in range(ends)]),
            ],
            axis=dim,
        )
    return cells


def rows_first(arrays, axis, dims):
    turned = [jnp.moveaxis(a, dim, 0) for a, dim in zip(arrays, dims)]
    both = jnp.concatenate([t.reshape(len(t), -1) for t in turned], axis=1)
    result, at, done = (lax.all_gather(both, axis, axis=0, tiled=True), 0, [])
    for t, dim in zip(turned, dims):
        slab = result[:, at : at + t[0].size].reshape(-1, *t.shape[1:])
        done.append(jnp.moveaxis(slab, 0, dim))
        at += t[0].size
    return tuple(done)


def extended_3(shard, sides, width):
    edges = {}
    for axis, dim in sides:
        devices, length = (lax.axis_size(axis), shard.shape[dim])
        up = [(i, (i + 1) % devices) for i in range(devices - 1)]
        last = lax.slice_in_dim(shard, length - width, length, axis=dim)
        first = lax.slice_in_dim(shard, 0, width, axis=dim)
        edges[dim] = (
            lax.ppermute(last, axis, up),
            lax.ppermute(first, axis, [(b, a) for a, b in up]),
        )
    done = []
    for _, dim in sides:
        low, high = edges[dim]
        around = [(width, width) if d in done else (0, 0) for d in range(shard.ndim)]
        shard = jnp.concatenate([jnp.pad(low, around), shard, jnp.pad(high, around)], axis=dim)
        done.append(dim)
    return shard


def over_axes_2(shard, axes):
    return functools.reduce(lax.psum, axes, shard)


def interp(padded, axis):
    length = padded.shape[axis] - 2
    before = lax.slice_in_dim(padded, 0, length, axis=axis)
    middle = lax.slice_in_dim(padded, 1, length + 1, axis=axis)
    after = lax.slice_in_dim(padded, 2, length + 2, axis=axis)
    even_part = 0.25 * before + 0.75 * middle
    odd_part = 0.75 * middle + 0.25 * after
    paired = jnp.stack([even_part, odd_part], axis + 1)
    new_shape = list(middle.shape)
    new_shape[axis] = 2 * length
    return paired.reshape(new_shape)


def conv_taps(taps_weight, padded, row_count, col_count):
    summed = None
    for row_tap in range(3):
        for col_tap in range(3):
            window = padded[:, :, row_tap : row_tap + row_count, col_tap : col_tap + col_count]
            term = jnp.einsum(
                "oc,ncrw->norw",
                taps_weight[row_tap, col_tap],
                window,
                preferred_element_type=jnp.float32,
            )
            summed = term if summed is None else summed + term
    return summed


def apply_norm(blocks, mean_value, variance, full_shape, gain, shift):
    scaled = (
        (blocks - mean_value[:, :, None]) * lax.rsqrt(variance[:, :, None] + epsilon)
    ).reshape(full_shape)
    return (
        scaled * gain.astype(jnp.float32)[None, :, None, None]
        + shift.astype(jnp.float32)[None, :, None, None]
    )


def per_device(
    fine_features,
    coarse_level,
    lat_weight,
    lat_gain,
    lat_shift,
    out_weight,
    out_gain,
    out_shift,
    mask_weight,
    mask_bias,
    queries,
):
    images, in_share, band_rows, columns = fine_features.shape
    out_share = lat_weight.shape[0]
    group_size = D // GROUPS
    band_count = lax.axis_size(BAND)
    pixel_count = float(group_size * band_rows * band_count * columns)
    lateral = jnp.einsum(
        "oc,ncrw->norw",
        lat_weight,
        whole_of(fine_features, CHAN, 1),
        preferred_element_type=jnp.float32,
    )
    lat_blocks = lateral.reshape(images, out_share // group_size, -1)
    first_sum, square_sum = together(
        (jnp.sum(lat_blocks, 2), jnp.sum(lat_blocks * lat_blocks, 2)), BAND
    )
    lat_mean = first_sum / pixel_count
    lat_var = square_sum / pixel_count - lat_mean * lat_mean
    lat_normed = apply_norm(lat_blocks, lat_mean, lat_var, lateral.shape, lat_gain, lat_shift)
    band_index = lax.axis_index(BAND)
    extended = extended_2(coarse_level, ((BAND, 2),), 1)
    top_row = jnp.where(band_index == 0, extended[:, :, 1:2], extended[:, :, 0:1])
    bottom_row = jnp.where(band_index == band_count - 1, extended[:, :, -2:-1], extended[:, :, -1:])
    extended = jnp.concatenate([top_row, extended[:, :, 1:-1], bottom_row], 2).astype(jnp.float32)
    extended = jnp.pad(extended, ((0, 0), (0, 0), (0, 0), (1, 1)), mode="edge")
    upsampled = interp(interp(extended, 2), 3)
    joined = (lat_normed + upsampled).astype(jnp.bfloat16)
    row_joined = lax.all_to_all(joined, CHAN, split_axis=2, concat_axis=1, tiled=True)
    conv_weight, full_gain, full_shift, full_mask, full_bias = rows_first(
        (out_weight, out_gain, out_shift, mask_weight, mask_bias), CHAN, (2, 0, 0, 0, 0)
    )
    row_count = row_joined.shape[2]
    padded = extended_3(row_joined, ((BAND_CHAN, 2),), 1)
    padded = jnp.pad(padded, ((0, 0), (0, 0), (0, 0), (1, 1)))
    conv_out = conv_taps(conv_weight, padded, row_count, columns)
    local_groups = conv_out.shape[1] // group_size
    conv_blocks = conv_out.reshape(images, local_groups, -1)
    first_sum, square_sum = (
        over_axes_2(jnp.sum(conv_blocks, 2), BAND_CHAN),
        over_axes_2(jnp.sum(conv_blocks * conv_blocks, 2), BAND_CHAN),
    )
    out_mean = first_sum / pixel_count
    out_var = square_sum / pixel_count - out_mean * out_mean
    activated = jnp.maximum(
        apply_norm(conv_blocks, out_mean, out_var, conv_out.shape, full_gain, full_shift), 0.0
    ).astype(jnp.bfloat16)
    mixed = jnp.einsum("oc,ncrw->norw", full_mask, activated, preferred_element_type=jnp.float32)
    features = (mixed + full_bias.astype(jnp.float32)[None, :, None, None]).astype(jnp.bfloat16)
    logits = jnp.einsum("qc,ncrw->nqrw", queries, features, preferred_element_type=jnp.float32)
    peak = jnp.max(logits, axis=1, keepdims=True)
    shifted = logits - peak
    return shifted - jnp.log(jnp.sum(jnp.exp(shifted), axis=1, keepdims=True))


def solution(mesh):
    finer = Mesh(
        mesh.devices.reshape(8, 2, 2, 4, 2), ("band_0", "band_1", "band_2", "chan_0", "chan_1")
    )
    return jax.shard_map(
        per_device,
        mesh=finer,
        in_specs=(
            P(None, CHAN, BAND, None),
            P(None, CHAN, BAND, None),
            P(CHAN, None),
            P(CHAN),
            P(CHAN),
            P(None, None, CHAN, None),
            P(CHAN),
            P(CHAN),
            P(CHAN, None),
            P(CHAN),
            P(),
        ),
        out_specs=P(None, None, BAND_CHAN, None),
        check_vma=False,
    )
```

profile of v0, /device:TPU:16, one launch (start us, length us, event | category | flops | bytes accessed | tf_op | source)
XLA Modules:
  0.0 195.7 jit_solution(14821775544528148993)
XLA Ops:
  6.6 1.3 copy.111
  7.9 11.8 %all_gather.9 = bf16[2,48,8,512]{3,1,2,0:T(8,128)(2,1)} all-gather(bf16[2,24,8,512]{3,1,2,0:T(8,128)(2,1)S(1)} %copy.111), channel_id=1, replica_groups=mesh['band_0'=8,'band_1'=2,'band_2'=2,'chan_0'=4,'chan_1'=2] {'chan_1'}, dimensions={1}, use_global_device_ids=true | all-gather | bytes 1179648 | tf_op jit(solution)/shard_map/all_gather | solution.py:18
  19.8 1.9 collective-permute-start
  21.7 5.1 %collective-permute-start.1 = (bf16[2,32,1,256]{3,1,2,0:T(8,128)(2,1)S(1)}, bf16[2,32,1,256]{3,1,2,0:T(8,128)(2,1)S(1)}, u32[]{:S(2)}, u32[]{:S(2)}) collective-permute-start(bf16[2,32,1,256]{3,1,2,0:T(8,128)(2,1)S(1)} %get-tuple-element.31), channel_id=1, source_target_pairs={{8,0},{16,8},{24,16},{32,24},{40,32},{48,40},{56,48},{64,56},{72,6... | collective-permute-start | bytes 98312 | tf_op jit(solution)/shard_map/ppermute | solution.py:53
  26.9 0.1 copy.127
  27.2 0.1 copy.126
  27.3 0.2 reshape.197
  27.5 0.8 concatenate.20
  28.5 0.1 fusion.51
  28.6 0.3 pad_maximum_fusion.2
  29.1 0.3 fusion.24
  29.4 35.2 %all-gather.3.cloned.1.call-done = bf16[2,192,8,512]{3,1,2,0:T(8,128)(2,1)} async-done(((bf16[2,48,8,512]{3,1,2,0:T(8,128)(2,1)}), bf16[2,192,8,512]{3,1,2,0:T(8,128)(2,1)}) %all-gather.3.cloned.1.call-update) | async-done | bytes 3145744 | tf_op jit(solution)/shard_map/all_gather | solution.py:18
  64.6 2.7 %fusion.50 = (f32[2,32]{1,0:T(2,128)S(1)}, f32[2,32]{1,0:T(2,128)S(1)}, f32[2,32,8,512]{3,1,2,0:T(8,128)S(1)}) fusion(bf16[2,192,8,512]{3,1,2,0:T(8,128)(2,1)} %all-gather.3.cloned.1.call-done, bf16[32,192]{1,0:T(8,128)(2,1)S(1)} %copy-done.5), kind=kOutput, calls=%fused_computation.91 | convolution fusion | flops 101449600 | bytes 4207104 | tf_op jit(solution)/shard_map/oc,ncrw->norw/dot_general | solution.py:151
  67.9 0.6 broadcast_in_dim.2
  68.5 10.1 %all-to-all-start = ((f32[32,1,16]{2,1,0:T(1,128)}), f32[32,1,16]{2,1,0:T(1,128)S(1)}, u32[]{:S(2)}, u32[]{:S(2)}) async-start(f32[32,1,16]{2,1,0:T(1,128)} %broadcast_in_dim.2), calls=%async_computation | async-start | bytes 32768 | tf_op jit(solution)/shard_map/all_to_all | solution.py:24
  78.7 0.1 pad_maximum_fusion
  78.8 3.7 %copy.119 = f32[2,32,8,256,2]{1,2,4,3,0:T(8,128)} copy(f32[2,32,8,256,2]{3,1,2,0,4:T(8,128)S(1)} %pad_maximum_fusion) | data formatting | bytes 2097152 | tf_op jit(solution)/shard_map/stack | solution.py:102
  82.4 2.8 %copy.120 = f32[2,32,8,512]{3,1,2,0:T(8,128)S(1)} copy(f32[2,32,8,512]{1,2,3,0:T(8,128)} %bitcast.154) | data formatting | bytes 2097152 | tf_op jit(solution)/shard_map/reshape | solution.py:105
  85.3 0.5 all-to-all-done
  86.4 0.4 add_convert_fusion
  86.8 14.9 %all_to_all.24 = bf16[2,32,8,512]{3,1,0,2:T(8,128)(2,1)S(1)} all-to-all(bf16[2,32,8,512]{3,1,0,2:T(8,128)(2,1)S(1)} %copy.121), channel_id=1, replica_groups=mesh['band_0'=8,'band_1'=2,'band_2'=2,'chan_0'=4,'chan_1'=2] {'chan_0','..., dimensions={2} | all-to-all | bytes 1048576 | tf_op jit(solution)/shard_map/all_to_all | solution.py:172
  101.7 1.0 copy.123
  102.7 5.3 %collective-permute-start.3 = (bf16[2,256,1,512]{1,3,0,2:T(8,128)(2,1)}, bf16[2,256,1,512]{1,3,0,2:T(8,128)(2,1)}, u32[]{:S(2)}, u32[]{:S(2)}) collective-permute-start(bf16[2,256,1,512]{1,3,0,2:T(8,128)(2,1)} %copy.123), channel_id=1, source_target_pairs={{1,0},{2,1},{3,2},{4,3},{5,4},{6,5},{7,6},{8,7},{9,8},{10,9},{11,1... | collective-permute-start | bytes 1572872 | tf_op jit(solution)/shard_map/ppermute | solution.py:80
  108.0 1.9 collective-permute-start.2
  110.0 18.9 %all-gather.5.cloned.1.call-done = bf16[256,2563]{1,0:T(8,128)(2,1)} async-done(((bf16[32,2563]{1,0:T(8,128)(2,1)}), bf16[256,2563]{1,0:T(8,128)(2,1)}) %all-gather.5.cloned.1.call-update) | async-done | bytes 1312272 | tf_op jit(solution)/shard_map/all_gather | solution.py:63
  128.9 1.3 slice-done
  130.2 0.6 copy.130
  130.8 1.6 copy.131
  132.4 0.2 convert_reduce_fusion.2
  132.6 1.3 fusion.44
  133.9 0.8 collective-permute-done.2
  134.7 1.7 fusion.5
  136.4 0.3 fusion.17
  136.7 0.3 fusion.18
  137.1 0.3 fusion.19
  137.4 0.3 fusion.20
  137.8 0.3 fusion.16
  138.1 1.4 fusion.27
  139.5 1.4 fusion.25
  140.8 1.6 fusion.49
  142.8 17.4 %all-reduce.1 = (f32[2,32]{1,0:T(2,128)S(1)}, f32[2,32]{1,0:T(2,128)S(1)}) all-reduce(f32[2,32]{1,0:T(2,128)S(1)} %reduce_sum.94, f32[2,32]{1,0:T(2,128)S(1)} %reduce_sum.91), channel_id=1, replica_groups=mesh['band_0'=8,'band_1'=2,'band_2'=2,'chan_0'=4,'chan_1'=2] {'band_0'}, use_global_device_ids=true, to_apply=%region_14.15 | all-reduce | flops 128 | bytes 1024 | tf_op jit(solution)/shard_map/psum | solution.py:92
  160.3 6.4 %all-reduce.5 = (f32[2,32]{1,0:T(2,128)S(1)}, f32[2,32]{1,0:T(2,128)S(1)}) all-reduce(f32[2,32]{1,0:T(2,128)S(1)} %get-tuple-element.12, f32[2,32]{1,0:T(2,128)S(1)} %get-tuple-element.13), channel_id=1, replica_groups=mesh['band_0'=8,'band_1'=2,'band_2'=2,'chan_0'=4,'chan_1'=2] {'band_1'}, use_global_device_ids=true, to_apply=%region_15.16 | all-reduce | flops 128 | bytes 1024 | tf_op jit(solution)/shard_map/psum | solution.py:92
  166.7 2.4 %all-reduce.4 = (f32[2,32]{1,0:T(2,128)S(1)}, f32[2,32]{1,0:T(2,128)S(1)}) all-reduce(f32[2,32]{1,0:T(2,128)S(1)} %get-tuple-element.20, f32[2,32]{1,0:T(2,128)S(1)} %get-tuple-element.21), channel_id=1, replica_groups=mesh['band_0'=8,'band_1'=2,'band_2'=2,'chan_0'=4,'chan_1'=2] {'band_2'}, use_global_device_ids=true, to_apply=%region_16.17 | all-reduce | flops 128 | bytes 1024 | tf_op jit(solution)/shard_map/psum | solution.py:92
  169.1 10.5 %all-reduce.2 = (f32[2,32]{1,0:T(2,128)S(1)}, f32[2,32]{1,0:T(2,128)S(1)}) all-reduce(f32[2,32]{1,0:T(2,128)S(1)} %get-tuple-element.18, f32[2,32]{1,0:T(2,128)S(1)} %get-tuple-element.19), channel_id=1, replica_groups=mesh['band_0'=8,'band_1'=2,'band_2'=2,'chan_0'=4,'chan_1'=2] {'chan_0'}, use_global_device_ids=true, to_apply=%region_17.18 | all-reduce | flops 128 | bytes 1024 | tf_op jit(solution)/shard_map/psum | solution.py:92
  179.6 4.9 %all-reduce.3 = (f32[2,32]{1,0:T(2,128)S(1)}, f32[2,32]{1,0:T(2,128)S(1)}) all-reduce(f32[2,32]{1,0:T(2,128)S(1)} %get-tuple-element.14, f32[2,32]{1,0:T(2,128)S(1)} %get-tuple-element.15), channel_id=1, replica_groups=mesh['band_0'=8,'band_1'=2,'band_2'=2,'chan_0'=4,'chan_1'=2] {'chan_1'}, use_global_device_ids=true, to_apply=%region_18.19 | all-reduce | flops 128 | bytes 1024 | tf_op jit(solution)/shard_map/psum | solution.py:92
  184.9 1.9 fusion.53
  186.8 0.1 exponential_reduce_fusion
  187.1 1.7 copy.134
  (71 shorter events, 2.8 us)
Async XLA Ops:
  6.5 178.3 %copy-start = (bf16[200,256]{1,0:T(8,128)(2,1)S(1)}, bf16[200,256]{1,0:T(8,128)(2,1)}, u32[]{:S(2)}) copy-start(bf16[200,256]{1,0:T(8,128)(2,1)} %param.21) | copy-start | bytes 307204
  6.5 13.2 %copy-start.4 = (bf16[2,32,4,256]{3,2,1,0:T(4,128)(2,1)S(1)}, bf16[2,32,4,256]{3,2,1,0:T(4,128)(2,1)}, u32[]{:S(2)}) copy-start(bf16[2,32,4,256]{3,2,1,0:T(4,128)(2,1)} %param.12) | copy-start | bytes 393220
  6.5 20.3 %copy-start.7 = (bf16[32]{0:T(256)(128)(2,1)S(1)}, bf16[32]{0:T(256)(128)(2,1)}, u32[]{:S(2)}) copy-start(bf16[32]{0:T(256)(128)(2,1)} %param.17) | copy-start | bytes 196
  6.5 20.4 %copy-start.8 = (bf16[32]{0:T(256)(128)(2,1)S(1)}, bf16[32]{0:T(256)(128)(2,1)}, u32[]{:S(2)}) copy-start(bf16[32]{0:T(256)(128)(2,1)} %param.18) | copy-start | bytes 196
  6.5 20.5 %copy-start.9 = (bf16[32]{0:T(256)(128)(2,1)S(1)}, bf16[32]{0:T(256)(128)(2,1)}, u32[]{:S(2)}) copy-start(bf16[32]{0:T(256)(128)(2,1)} %param.20) | copy-start | bytes 196
  6.5 20.6 %copy-start.3 = (bf16[3,3,32,256]{3,2,1,0:T(8,128)(2,1)S(1)}, bf16[3,3,32,256]{3,2,1,0:T(8,128)(2,1)}, u32[]{:S(2)}) copy-start(bf16[3,3,32,256]{3,2,1,0:T(8,128)(2,1)} %param.16) | copy-start | bytes 442372
  6.6 58.1 %all-gather.3.cloned.1.call-start = ((), (), s32[]{:S(2)}) async-start(), calls=%async_computation.2 | async-start | bytes 3932160 | tf_op jit(solution)/shard_map/all_gather | solution.py:18
  7.9 19.6 %copy-start.6 = (bf16[32,256]{1,0:T(8,128)(2,1)S(1)}, bf16[32,256]{1,0:T(8,128)(2,1)}, u32[]{:S(2)}) copy-start(bf16[32,256]{1,0:T(8,128)(2,1)} %param.19) | copy-start | bytes 49156
  7.9 20.4 %copy-start.10 = (bf16[32]{0:T(256)(128)(2,1)S(1)}, bf16[32]{0:T(256)(128)(2,1)}, u32[]{:S(2)}) copy-start(bf16[32]{0:T(256)(128)(2,1)} %param.14) | copy-start | bytes 196
  7.9 20.4 %copy-start.11 = (bf16[32]{0:T(256)(128)(2,1)S(1)}, bf16[32]{0:T(256)(128)(2,1)}, u32[]{:S(2)}) copy-start(bf16[32]{0:T(256)(128)(2,1)} %param.15) | copy-start | bytes 196
  19.7 109.2 %all-gather.5.cloned.1.call-start = ((), (), s32[]{:S(2)}) async-start(), calls=%async_computation.3 | async-start | bytes 1548288 | tf_op jit(solution)/shard_map/all_gather | solution.py:63
  19.8 8.6 %collective-permute-start = (bf16[2,32,1,256]{3,1,2,0:T(8,128)(2,1)S(1)}, bf16[2,32,1,256]{3,1,2,0:T(8,128)(2,1)S(1)}, u32[]{:S(2)}, u32[]{:S(2)}) collective-permute-start(bf16[2,32,1,256]{3,1,2,0:T(8,128)(2,1)S(1)} %get-tuple-element.30), channel_id=1, source_target_pairs={{0,8},{8,16},{16,24},{24,32},{32,40},{40,48},{48,56},{56,64},{64,7... | collective-permute-start | bytes 98312 | tf_op jit(solution)/shard_map/ppermute | solution.py:51
  21.7 6.7 %collective-permute-start.1 = (bf16[2,32,1,256]{3,1,2,0:T(8,128)(2,1)S(1)}, bf16[2,32,1,256]{3,1,2,0:T(8,128)(2,1)S(1)}, u32[]{:S(2)}, u32[]{:S(2)}) collective-permute-start(bf16[2,32,1,256]{3,1,2,0:T(8,128)(2,1)S(1)} %get-tuple-element.31), channel_id=1, source_target_pairs={{8,0},{16,8},{24,16},{32,24},{40,32},{48,40},{56,48},{64,56},{72,6... | collective-permute-start | bytes 98312 | tf_op jit(solution)/shard_map/ppermute | solution.py:53
  29.1 35.6 %copy-start.5 = (bf16[32,192]{1,0:T(8,128)(2,1)S(1)}, bf16[32,192]{1,0:T(8,128)(2,1)}, u32[]{:S(2)}) copy-start(bf16[32,192]{1,0:T(8,128)(2,1)} %param.13) | copy-start | bytes 36868
  68.5 17.2 %all-to-all-start = ((f32[32,1,16]{2,1,0:T(1,128)}), f32[32,1,16]{2,1,0:T(1,128)S(1)}, u32[]{:S(2)}, u32[]{:S(2)}) async-start(f32[32,1,16]{2,1,0:T(1,128)} %broadcast_in_dim.2), calls=%async_computation | async-start | bytes 32768 | tf_op jit(solution)/shard_map/all_to_all | solution.py:24
  102.7 31.1 %collective-permute-start.3 = (bf16[2,256,1,512]{1,3,0,2:T(8,128)(2,1)}, bf16[2,256,1,512]{1,3,0,2:T(8,128)(2,1)}, u32[]{:S(2)}, u32[]{:S(2)}) collective-permute-start(bf16[2,256,1,512]{1,3,0,2:T(8,128)(2,1)} %copy.123), channel_id=1, source_target_pairs={{1,0},{2,1},{3,2},{4,3},{5,4},{6,5},{7,6},{8,7},{9,8},{10,9},{11,1... | collective-permute-start | bytes 1572872 | tf_op jit(solution)/shard_map/ppermute | solution.py:80
  108.0 26.6 %collective-permute-start.2 = (bf16[2,256,1,512]{1,3,0,2:T(8,128)(2,1)}, bf16[2,256,1,512]{1,3,0,2:T(8,128)(2,1)}, u32[]{:S(2)}, u32[]{:S(2)}) collective-permute-start(bf16[2,256,1,512]{1,3,0,2:T(8,128)(2,1)} %copy.123), channel_id=1, source_target_pairs={{0,1},{1,2},{2,3},{3,4},{4,5},{5,6},{6,7},{7,8},{8,9},{9,10},{10,1... | collective-permute-start | bytes 1572872 | tf_op jit(solution)/shard_map/ppermute | solution.py:79
  128.9 1.3 slice-start
  130.8 1.6 copy-start.1
  133.8 2.6 %copy-start.2 = (bf16[256,3,3,256]{3,0,2,1:T(8,128)(2,1)S(1)}, bf16[256,3,3,256]{3,0,2,1:T(8,128)(2,1)}, u32[]{:S(2)}) copy-start(bf16[256,3,3,256]{3,0,2,1:T(8,128)(2,1)} %copy.131) | copy-start | bytes 3538948
Sparse Core Ops, SparseCore 0:
  19.8 44.7 all-gather.2
  66.4 62.4 all-gather.4
where the time goes:
time: 196 us
  blocking collectives  68.3 us (35%)
  waiting for transfers between devices  55.6 us (28%)
  starting transfers between devices  24.5 us (12%)
  local copies, waits for them, and re-layouts  17.5 us (9%)
  between operations  13.8 us (7%)
  matrix products  11.9 us (6%)
  other arithmetic  4.01 us (2%)
    psum x5, blocking collectives, over_axes_2(): return functools.reduce(lax.psum, axes, shard)  41.7 us
    all_gather x1, waiting for transfers between devices, whole_of(): shard = lax.all_gather(shard, axis, axis=dim, tiled=True)  35.2 us
    all_gather x1, waiting for transfers between devices, rows_first(): result, at, done = (lax.all_gather(both, axis, axis=0, tiled=True), 0, [])  18.9 us
    all_to_all x1, blocking collectives, per_device(): lax.all_to_all(joined, CHAN, split_axis=2, concat_axis=1, tiled=True)  14.9 us
    all_gather x1, blocking collectives, whole_of(): shard = lax.all_gather(shard, axis, axis=dim, tiled=True)  11.8 us
    all_to_all x1, starting transfers between devices, from_everyone(): lax.all_to_all(jnp.broadcast_to(shard[None], (devices, *shard.shape)), ax...  10.1 us
    dot_general x9, matrix products, conv_taps(): jnp.einsum('oc,ncrw->norw', taps_weight[row_tap, col_tap], window, prefer...  7.3 us
    ppermute x1, starting transfers between devices, extended_3(): lax.ppermute(first, axis, [(b, a) for a, b in up])  5.31 us
  transfers between devices with their start and end apart: 7, of which 5 were waited for; matrix products, arithmetic and copies ran while one was open for 9% of the time, Pallas kernels for 0%

commit v1 on v0

--- a/solution.py
+++ b/solution.py
@@ -60,7 +60,13 @@
 def rows_first(arrays, axis, dims):
     turned = [jnp.moveaxis(a, dim, 0) for a, dim in zip(arrays, dims)]
     both = jnp.concatenate([t.reshape(len(t), -1) for t in turned], axis=1)
-    result, at, done = (lax.all_gather(both, axis, axis=0, tiled=True), 0, [])
+    result, at, done = (
+        jnp.concatenate(
+            lax.all_to_all(jnp.stack([both] * lax.axis_size(axis)), axis, 0, 0), axis=0
+        ),
+        0,
+        [],
+    )
     for t, dim in zip(turned, dims):
         slab = result[:, at : at + t[0].size].reshape(-1, *t.shape[1:])
         done.append(jnp.moveaxis(slab, 0, dim))

time: 196 us -> 204 us (1.041)
  blocking collectives: 68.3 us -> 55.1 us
  waiting for transfers between devices: 55.6 us -> 68 us
  starting transfers between devices: 24.5 us -> 32.6 us
  matrix products: 11.9 us -> 9.78 us
    all_to_all x0 -> x2, waiting for transfers between devices: none -> 19.1 us  [the longest x1 10.5 us: rows_first(): lax.all_to_all(jnp.stack([both] * lax.axis_size(axis)), axis, 0, 0)]
    all_gather x1 -> x0, waiting for transfers between devices: 18.9 us -> none  [rows_first(): result, at, done = (lax.all_gather(both, axis, axis=0, tiled=True), 0, [])]
    all_to_all x1 -> x0, blocking collectives: 14.9 us -> none  [per_device(): lax.all_to_all(joined, CHAN, split_axis=2, concat_axis=1, tiled=True)]
    ppermute x1, waiting for transfers between devices: 0.01 us -> 8.23 us  [extended_3(): lax.ppermute(first, axis, [(b, a) for a, b in up])]
    all_to_all x0 -> x2, starting transfers between devices: none -> 7.39 us  [the longest x1 3.82 us: per_device(): lax.all_to_all(joined, CHAN, split_axis=2, concat_axis=1, tiled=True)]
    ppermute x1, waiting for transfers between devices: 0.81 us -> 3.29 us  [extended_3(): lax.ppermute(last, axis, up)]
  transfers between devices with their start and end apart: 7 -> 8, of which waited for: 5 -> 7; matrix products, arithmetic and copies ran while one was open for 9% -> 7% of each run, Pallas kernels for 0% -> 0%
where the time goes in v1:
time: 204 us; the launch traced here: 203 us
  waiting for transfers between devices  68 us (33%)
  blocking collectives  55.1 us (27%)
  starting transfers between devices  32.6 us (16%)
  local copies, waits for them, and re-layouts  19.5 us (10%)
  between operations  13.8 us (7%)
  matrix products  9.78 us (5%)
  other arithmetic  4 us (2%)
    psum x5, blocking collectives, over_axes_2(): return functools.reduce(lax.psum, axes, shard)  43.5 us
    all_gather x1, waiting for transfers between devices, whole_of(): shard = lax.all_gather(shard, axis, axis=dim, tiled=True)  35.3 us
    all_gather x1, blocking collectives, whole_of(): shard = lax.all_gather(shard, axis, axis=dim, tiled=True)  11.6 us
    all_to_all x1, waiting for transfers between devices, rows_first(): lax.all_to_all(jnp.stack([both] * lax.axis_size(axis)), axis, 0, 0)  10.5 us
    all_to_all x1, starting transfers between devices, from_everyone(): lax.all_to_all(jnp.broadcast_to(shard[None], (devices, *shard.shape)), ax...  10.1 us
    all_to_all x1, waiting for transfers between devices, per_device(): lax.all_to_all(joined, CHAN, split_axis=2, concat_axis=1, tiled=True)  8.61 us
    ppermute x1, waiting for transfers between devices, extended_3(): lax.ppermute(first, axis, [(b, a) for a, b in up])  8.23 us
    dot_general x9, matrix products, conv_taps(): jnp.einsum('oc,ncrw->norw', taps_weight[row_tap, col_tap], window, prefer...  6.4 us
  transfers between devices with their start and end apart: 8, of which 7 were waited for; matrix products, arithmetic and copies ran while one was open for 7% of the time, Pallas kernels for 0%

profile of v1, /device:TPU:16, one launch (start us, length us, event | category | flops | bytes accessed | tf_op | source)
XLA Modules:
  0.0 202.8 jit_solution(12916896906545350610)
XLA Ops:
  6.6 1.2 copy.110
  7.8 11.6 %all_gather.6 = bf16[2,48,8,512]{3,1,2,0:T(8,128)(2,1)} all-gather(bf16[2,24,8,512]{3,1,2,0:T(8,128)(2,1)S(1)} %copy.110), channel_id=1, replica_groups=mesh['band_0'=8,'band_1'=2,'band_2'=2,'chan_0'=4,'chan_1'=2] {'chan_1'}, dimensions={1}, use_global_device_ids=true | all-gather | bytes 1179648 | tf_op jit(solution)/shard_map/all_gather | solution.py:18
  19.5 1.9 collective-permute-start
  21.4 5.1 %collective-permute-start.1 = (bf16[2,32,1,256]{3,1,2,0:T(8,128)(2,1)S(1)}, bf16[2,32,1,256]{3,1,2,0:T(8,128)(2,1)S(1)}, u32[]{:S(2)}, u32[]{:S(2)}) collective-permute-start(bf16[2,32,1,256]{3,1,2,0:T(8,128)(2,1)S(1)} %get-tuple-element.31), channel_id=1, source_target_pairs={{8,0},{16,8},{24,16},{32,24},{40,32},{48,40},{56,48},{64,56},{72,6... | collective-permute-start | bytes 98312 | tf_op jit(solution)/shard_map/ppermute | solution.py:53
  26.6 1.5 collective-permute-done.1
  28.3 0.3 pad_maximum_fusion.2
  28.8 0.3 fusion.24
  29.1 35.3 %all-gather.2.cloned.1.call-done = bf16[2,192,8,512]{3,1,2,0:T(8,128)(2,1)} async-done(((bf16[2,48,8,512]{3,1,2,0:T(8,128)(2,1)}), bf16[2,192,8,512]{3,1,2,0:T(8,128)(2,1)}) %all-gather.2.cloned.1.call-update) | async-done | bytes 3145744 | tf_op jit(solution)/shard_map/all_gather | solution.py:18
  64.4 2.7 %fusion.50 = (f32[2,32]{1,0:T(2,128)S(1)}, f32[2,32]{1,0:T(2,128)S(1)}, f32[2,32,8,512]{3,1,2,0:T(8,128)S(1)}) fusion(bf16[2,192,8,512]{3,1,2,0:T(8,128)(2,1)} %all-gather.2.cloned.1.call-done, bf16[32,192]{1,0:T(8,128)(2,1)S(1)} %copy-done.4), kind=kOutput, calls=%fused_computation.91 | convolution fusion | flops 101449600 | bytes 4207104 | tf_op jit(solution)/shard_map/oc,ncrw->norw/dot_general | solution.py:157
  67.7 0.6 broadcast_in_dim.2
  68.3 10.1 %all-to-all-start = ((f32[32,1,16]{2,1,0:T(1,128)}), f32[32,1,16]{2,1,0:T(1,128)S(1)}, u32[]{:S(2)}, u32[]{:S(2)}) async-start(f32[32,1,16]{2,1,0:T(1,128)} %broadcast_in_dim.2), calls=%async_computation | async-start | bytes 32768 | tf_op jit(solution)/shard_map/all_to_all | solution.py:24
  78.5 3.7 %copy.118 = f32[2,32,8,256,2]{1,2,4,3,0:T(8,128)} copy(f32[2,32,8,256,2]{3,1,2,0,4:T(8,128)S(1)} %pad_maximum_fusion) | data formatting | bytes 2097152 | tf_op jit(solution)/shard_map/stack | solution.py:108
  82.2 2.8 %copy.119 = f32[2,32,8,512]{3,1,2,0:T(8,128)S(1)} copy(f32[2,32,8,512]{1,2,3,0:T(8,128)} %bitcast.155) | data formatting | bytes 2097152 | tf_op jit(solution)/shard_map/reshape | solution.py:111
  85.0 0.5 all-to-all-done
  86.1 0.4 add_convert_fusion
  86.6 0.8 copy.120
  87.4 3.8 %all-to-all-start.1 = ((bf16[2,32,8,512]{3,1,0,2:T(8,128)(2,1)}), bf16[2,32,8,512]{3,1,0,2:T(8,128)(2,1)S(1)}, u32[]{:S(2)}, u32[]{:S(2)}) async-start(bf16[2,32,8,512]{3,1,0,2:T(8,128)(2,1)} %copy.120), calls=%async_computation.1 | async-start | bytes 1048576 | tf_op jit(solution)/shard_map/all_to_all | solution.py:178
  91.7 0.2 reshape.202
  91.9 8.6 %all-to-all-done.1 = bf16[2,32,8,512]{3,1,0,2:T(8,128)(2,1)S(1)} async-done(((bf16[2,32,8,512]{3,1,0,2:T(8,128)(2,1)}), bf16[2,32,8,512]{3,1,0,2:T(8,128)(2,1)S(1)}, u32[]{:S(2)}, u32[]{:S(2)}) %all-to-all-start.1) | async-done | bytes 524320 | tf_op jit(solution)/shard_map/all_to_all | solution.py:178
  100.6 1.2 stack.35
  101.7 3.6 %all-to-all-start.2 = ((bf16[8,32,2563]{2,1,0:T(8,128)(2,1)}), bf16[8,32,2563]{2,1,0:T(8,128)(2,1)S(1)}, u32[]{:S(2)}, u32[]{:S(2)}) async-start(bf16[8,32,2563]{2,1,0:T(8,128)(2,1)} %stack.35), calls=%async_computation.2 | async-start | bytes 2752512 | tf_op jit(solution)/shard_map/all_to_all | solution.py:65
  105.4 1.0 copy.122
  106.4 6.1 %collective-permute-start.3 = (bf16[2,256,1,512]{1,3,0,2:T(8,128)(2,1)}, bf16[2,256,1,512]{1,3,0,2:T(8,128)(2,1)}, u32[]{:S(2)}, u32[]{:S(2)}) collective-permute-start(bf16[2,256,1,512]{1,3,0,2:T(8,128)(2,1)} %copy.122), channel_id=1, source_target_pairs={{1,0},{2,1},{3,2},{4,3},{5,4},{6,5},{7,6},{8,7},{9,8},{10,9},{11,1... | collective-permute-start | bytes 1572872 | tf_op jit(solution)/shard_map/ppermute | solution.py:86
  112.5 1.9 collective-permute-start.2
  114.4 10.5 %all-to-all-done.2 = bf16[8,32,2563]{2,1,0:T(8,128)(2,1)S(1)} async-done(((bf16[8,32,2563]{2,1,0:T(8,128)(2,1)}), bf16[8,32,2563]{2,1,0:T(8,128)(2,1)S(1)}, u32[]{:S(2)}, u32[]{:S(2)}) %all-to-all-start.2) | async-done | bytes 1312288 | tf_op jit(solution)/shard_map/all_to_all | solution.py:65
  124.9 1.1 slice.167
  126.0 1.6 copy.129
  127.6 1.6 copy.130
  129.1 0.2 convert_reduce_fusion.2
  129.3 1.3 fusion.44
  130.6 8.2 %collective-permute-done.3 = bf16[2,256,1,512]{1,3,0,2:T(8,128)(2,1)} collective-permute-done((bf16[2,256,1,512]{1,3,0,2:T(8,128)(2,1)}, bf16[2,256,1,512]{1,3,0,2:T(8,128)(2,1)}, u32[]{:S(2)}, u32[]{:S(2)}) %collective-permute-start.3) | collective-permute-done | bytes 524320 | tf_op jit(solution)/shard_map/ppermute | solution.py:86
  138.8 3.3 %collective-permute-done.2 = bf16[2,256,1,512]{1,3,0,2:T(8,128)(2,1)} collective-permute-done((bf16[2,256,1,512]{1,3,0,2:T(8,128)(2,1)}, bf16[2,256,1,512]{1,3,0,2:T(8,128)(2,1)}, u32[]{:S(2)}, u32[]{:S(2)}) %collective-permute-start.2) | collective-permute-done | bytes 524320 | tf_op jit(solution)/shard_map/ppermute | solution.py:85
  142.1 1.7 fusion.5
  143.9 0.3 fusion.17
  144.2 0.3 fusion.18
  144.5 0.4 fusion.19
  144.9 0.3 fusion.20
  145.2 0.3 fusion.16
  145.6 1.4 fusion.27
  146.9 1.4 fusion.25
  148.3 0.7 fusion.49
  149.4 17.2 %all-reduce.1 = (f32[2,32]{1,0:T(2,128)S(1)}, f32[2,32]{1,0:T(2,128)S(1)}) all-reduce(f32[2,32]{1,0:T(2,128)S(1)} %reduce_sum.94, f32[2,32]{1,0:T(2,128)S(1)} %reduce_sum.91), channel_id=1, replica_groups=mesh['band_0'=8,'band_1'=2,'band_2'=2,'chan_0'=4,'chan_1'=2] {'band_0'}, use_global_device_ids=true, to_apply=%region_14.15 | all-reduce | flops 128 | bytes 1024 | tf_op jit(solution)/shard_map/psum | solution.py:98
  166.6 6.4 %all-reduce.5 = (f32[2,32]{1,0:T(2,128)S(1)}, f32[2,32]{1,0:T(2,128)S(1)}) all-reduce(f32[2,32]{1,0:T(2,128)S(1)} %get-tuple-element.12, f32[2,32]{1,0:T(2,128)S(1)} %get-tuple-element.13), channel_id=1, replica_groups=mesh['band_0'=8,'band_1'=2,'band_2'=2,'chan_0'=4,'chan_1'=2] {'band_1'}, use_global_device_ids=true, to_apply=%region_15.16 | all-reduce | flops 128 | bytes 1024 | tf_op jit(solution)/shard_map/psum | solution.py:98
  173.0 2.4 %all-reduce.4 = (f32[2,32]{1,0:T(2,128)S(1)}, f32[2,32]{1,0:T(2,128)S(1)}) all-reduce(f32[2,32]{1,0:T(2,128)S(1)} %get-tuple-element.20, f32[2,32]{1,0:T(2,128)S(1)} %get-tuple-element.21), channel_id=1, replica_groups=mesh['band_0'=8,'band_1'=2,'band_2'=2,'chan_0'=4,'chan_1'=2] {'band_2'}, use_global_device_ids=true, to_apply=%region_16.17 | all-reduce | flops 128 | bytes 1024 | tf_op jit(solution)/shard_map/psum | solution.py:98
  175.4 12.5 %all-reduce.2 = (f32[2,32]{1,0:T(2,128)S(1)}, f32[2,32]{1,0:T(2,128)S(1)}) all-reduce(f32[2,32]{1,0:T(2,128)S(1)} %get-tuple-element.18, f32[2,32]{1,0:T(2,128)S(1)} %get-tuple-element.19), channel_id=1, replica_groups=mesh['band_0'=8,'band_1'=2,'band_2'=2,'chan_0'=4,'chan_1'=2] {'chan_0'}, use_global_device_ids=true, to_apply=%region_17.18 | all-reduce | flops 128 | bytes 1024 | tf_op jit(solution)/shard_map/psum | solution.py:98
  188.0 4.9 %all-reduce.3 = (f32[2,32]{1,0:T(2,128)S(1)}, f32[2,32]{1,0:T(2,128)S(1)}) all-reduce(f32[2,32]{1,0:T(2,128)S(1)} %get-tuple-element.14, f32[2,32]{1,0:T(2,128)S(1)} %get-tuple-element.15), channel_id=1, replica_groups=mesh['band_0'=8,'band_1'=2,'band_2'=2,'chan_0'=4,'chan_1'=2] {'chan_1'}, use_global_device_ids=true, to_apply=%region_18.19 | all-reduce | flops 128 | bytes 1024 | tf_op jit(solution)/shard_map/psum | solution.py:98
  193.3 0.7 fusion.53
  194.2 1.7 copy.133
  (69 shorter events, 3.3 us)
Async XLA Ops:
  6.5 186.7 %copy-start = (bf16[200,256]{1,0:T(8,128)(2,1)S(1)}, bf16[200,256]{1,0:T(8,128)(2,1)}, u32[]{:S(2)}) copy-start(bf16[200,256]{1,0:T(8,128)(2,1)} %param.21) | copy-start | bytes 307204
  6.5 12.9 %copy-start.3 = (bf16[2,32,4,256]{3,2,1,0:T(4,128)(2,1)S(1)}, bf16[2,32,4,256]{3,2,1,0:T(4,128)(2,1)}, u32[]{:S(2)}) copy-start(bf16[2,32,4,256]{3,2,1,0:T(4,128)(2,1)} %param.12) | copy-start | bytes 393220
  6.5 20.0 %copy-start.9 = (bf16[32]{0:T(256)(128)(2,1)S(1)}, bf16[32]{0:T(256)(128)(2,1)}, u32[]{:S(2)}) copy-start(bf16[32]{0:T(256)(128)(2,1)} %param.14) | copy-start | bytes 196
  6.5 20.1 %copy-start.10 = (bf16[32]{0:T(256)(128)(2,1)S(1)}, bf16[32]{0:T(256)(128)(2,1)}, u32[]{:S(2)}) copy-start(bf16[32]{0:T(256)(128)(2,1)} %param.15) | copy-start | bytes 196
  6.5 57.8 %all-gather.2.cloned.1.call-start = ((), (), s32[]{:S(2)}) async-start(), calls=%async_computation.3 | async-start | bytes 3932160 | tf_op jit(solution)/shard_map/all_gather | solution.py:18
  19.5 7.1 %collective-permute-start = (bf16[2,32,1,256]{3,1,2,0:T(8,128)(2,1)S(1)}, bf16[2,32,1,256]{3,1,2,0:T(8,128)(2,1)S(1)}, u32[]{:S(2)}, u32[]{:S(2)}) collective-permute-start(bf16[2,32,1,256]{3,1,2,0:T(8,128)(2,1)S(1)} %get-tuple-element.30), channel_id=1, source_target_pairs={{0,8},{8,16},{16,24},{24,32},{32,40},{40,48},{48,56},{56,64},{64,7... | collective-permute-start | bytes 98312 | tf_op jit(solution)/shard_map/ppermute | solution.py:51
  21.4 6.7 %collective-permute-start.1 = (bf16[2,32,1,256]{3,1,2,0:T(8,128)(2,1)S(1)}, bf16[2,32,1,256]{3,1,2,0:T(8,128)(2,1)S(1)}, u32[]{:S(2)}, u32[]{:S(2)}) collective-permute-start(bf16[2,32,1,256]{3,1,2,0:T(8,128)(2,1)S(1)} %get-tuple-element.31), channel_id=1, source_target_pairs={{8,0},{16,8},{24,16},{32,24},{40,32},{48,40},{56,48},{64,56},{72,6... | collective-permute-start | bytes 98312 | tf_op jit(solution)/shard_map/ppermute | solution.py:53
  28.8 35.6 %copy-start.4 = (bf16[32,192]{1,0:T(8,128)(2,1)S(1)}, bf16[32,192]{1,0:T(8,128)(2,1)}, u32[]{:S(2)}) copy-start(bf16[32,192]{1,0:T(8,128)(2,1)} %param.13) | copy-start | bytes 36868
  68.3 17.2 %all-to-all-start = ((f32[32,1,16]{2,1,0:T(1,128)}), f32[32,1,16]{2,1,0:T(1,128)S(1)}, u32[]{:S(2)}, u32[]{:S(2)}) async-start(f32[32,1,16]{2,1,0:T(1,128)} %broadcast_in_dim.2), calls=%async_computation | async-start | bytes 32768 | tf_op jit(solution)/shard_map/all_to_all | solution.py:24
  86.5 4.7 %copy-start.6 = (bf16[32]{0:T(256)(128)(2,1)S(1)}, bf16[32]{0:T(256)(128)(2,1)}, u32[]{:S(2)}) copy-start(bf16[32]{0:T(256)(128)(2,1)} %param.17) | copy-start | bytes 196
  86.5 4.8 %copy-start.7 = (bf16[32]{0:T(256)(128)(2,1)S(1)}, bf16[32]{0:T(256)(128)(2,1)}, u32[]{:S(2)}) copy-start(bf16[32]{0:T(256)(128)(2,1)} %param.18) | copy-start | bytes 196
  86.5 4.9 %copy-start.8 = (bf16[32]{0:T(256)(128)(2,1)S(1)}, bf16[32]{0:T(256)(128)(2,1)}, u32[]{:S(2)}) copy-start(bf16[32]{0:T(256)(128)(2,1)} %param.20) | copy-start | bytes 196
  86.5 5.0 %copy-start.2 = (bf16[3,3,32,256]{3,2,1,0:T(8,128)(2,1)S(1)}, bf16[3,3,32,256]{3,2,1,0:T(8,128)(2,1)}, u32[]{:S(2)}) copy-start(bf16[3,3,32,256]{3,2,1,0:T(8,128)(2,1)} %param.16) | copy-start | bytes 442372
  86.5 5.3 %copy-start.5 = (bf16[32,256]{1,0:T(8,128)(2,1)S(1)}, bf16[32,256]{1,0:T(8,128)(2,1)}, u32[]{:S(2)}) copy-start(bf16[32,256]{1,0:T(8,128)(2,1)} %param.19) | copy-start | bytes 49156
  87.4 13.2 %all-to-all-start.1 = ((bf16[2,32,8,512]{3,1,0,2:T(8,128)(2,1)}), bf16[2,32,8,512]{3,1,0,2:T(8,128)(2,1)S(1)}, u32[]{:S(2)}, u32[]{:S(2)}) async-start(bf16[2,32,8,512]{3,1,0,2:T(8,128)(2,1)} %copy.120), calls=%async_computation.1 | async-start | bytes 1048576 | tf_op jit(solution)/shard_map/all_to_all | solution.py:178
  101.7 23.2 %all-to-all-start.2 = ((bf16[8,32,2563]{2,1,0:T(8,128)(2,1)}), bf16[8,32,2563]{2,1,0:T(8,128)(2,1)S(1)}, u32[]{:S(2)}, u32[]{:S(2)}) async-start(bf16[8,32,2563]{2,1,0:T(8,128)(2,1)} %stack.35), calls=%async_computation.2 | async-start | bytes 2752512 | tf_op jit(solution)/shard_map/all_to_all | solution.py:65
  106.4 32.5 %collective-permute-start.3 = (bf16[2,256,1,512]{1,3,0,2:T(8,128)(2,1)}, bf16[2,256,1,512]{1,3,0,2:T(8,128)(2,1)}, u32[]{:S(2)}, u32[]{:S(2)}) collective-permute-start(bf16[2,256,1,512]{1,3,0,2:T(8,128)(2,1)} %copy.122), channel_id=1, source_target_pairs={{1,0},{2,1},{3,2},{4,3},{5,4},{6,5},{7,6},{8,7},{9,8},{10,9},{11,1... | collective-permute-start | bytes 1572872 | tf_op jit(solution)/shard_map/ppermute | solution.py:86
  112.5 29.7 %collective-permute-start.2 = (bf16[2,256,1,512]{1,3,0,2:T(8,128)(2,1)}, bf16[2,256,1,512]{1,3,0,2:T(8,128)(2,1)}, u32[]{:S(2)}, u32[]{:S(2)}) collective-permute-start(bf16[2,256,1,512]{1,3,0,2:T(8,128)(2,1)} %copy.122), channel_id=1, source_target_pairs={{0,1},{1,2},{2,3},{3,4},{4,5},{5,6},{6,7},{7,8},{8,9},{9,10},{10,1... | collective-permute-start | bytes 1572872 | tf_op jit(solution)/shard_map/ppermute | solution.py:85
  130.6 13.3 %copy-start.1 = (bf16[256,3,3,256]{3,0,2,1:T(8,128)(2,1)S(1)}, bf16[256,3,3,256]{3,0,2,1:T(8,128)(2,1)}, u32[]{:S(2)}) copy-start(bf16[256,3,3,256]{3,0,2,1:T(8,128)(2,1)} %copy.130) | copy-start | bytes 3538948
Sparse Core Ops, SparseCore 0:
  19.6 44.7 all-gather.1
